TPU v7x, 256 devices: a 4x2x16 block of a 4x16x16 slice. The times are simulated.
256 devices in a mesh: grp: 2 (over y), row: 32 (over z, core), col: 4 (over x).
Axes of the slice: x: 4, y: 2, z: 16, core: 2. Of those that a mesh axis runs over, the one named last changes fastest.
The devices are a block of a 4x16x16 slice.
Arguments:
- pair: bfloat16 [768, 384, 128], P(('grp', 'row'), 'col'), parts along dimension 0, may hold values from -6 to 6
- token_count: int32 [2], P('grp'), parts along dimension 0, may hold values from 288 to 384
- tri_in: bfloat16 [2, 128, 512], replicated, may hold values from -0.5 to 0.5
- tri_gate: bfloat16 [2, 128, 128], replicated, may hold values from -0.5 to 0.5
- tri_out: bfloat16 [2, 128, 128], replicated, may hold values from -0.5 to 0.5
- trans_in: bfloat16 [128, 1024], replicated, may hold values from -0.5 to 0.5
- trans_out: bfloat16 [512, 128], replicated, may hold values from -0.25 to 0.25
Outputs:
- pair_out: bfloat16 [768, 384, 128], P(('grp', 'row'), 'col'), parts along dimension 0
There are 2 independent parts, one for each index of `grp`. A program takes and returns all parts, laid end to end along the dimension named above; an argument that names none is the same for every part. Nothing has to cross between parts.
Inputs may be any that keep to these rules, and one draw needn't show every extreme that they name: `token_count`: the number of real tokens of the complex; pair entries with either token index at or past it are padding.
All inputs are finite; a program needn't handle non-finite values.
Results may differ from a plain program's by a relative error of at most 0.015.
Values may be sent and summed in bfloat16 or wider, within the bound.
A program may use at most 64 MiB of HBM per device.

v0:
```python
import functools

import jax
import jax.numpy as jnp
from jax import lax
from jax.experimental import pallas as pl
from jax.experimental.pallas import tpu as pltpu
from jax.sharding import Mesh
from jax.sharding import PartitionSpec as P

MESH = pl.DeviceIdType.MESH
F32, BF16 = jnp.float32, jnp.bfloat16
CORES = 2
PIECES = 3


def log2(n):
    assert n & (n - 1) == 0
    return n.bit_length() - 1


def dot(a, b, ca, cb):
    return lax.dot_general(a, b, (((ca,), (cb,)), ((), ())), preferred_element_type=F32)


def layer_norm(v):
    average = jnp.mean(v, axis=0, keepdims=True)
    centred = v - average
    spread = jnp.mean(centred * centred, axis=0, keepdims=True)
    return centred * lax.rsqrt(spread + 1e-05)


def one_hot(shape, source_of_row):
    row = lax.broadcasted_iota(jnp.int32, shape, 0)
    col = lax.broadcasted_iota(jnp.int32, shape, 1)
    return (source_of_row(row) == col).astype(F32).astype(BF16)


def kernel(
    dims, count_ref, pair_ref, tri_in_ref, tri_gate_ref, tri_out_ref, trans_in_ref, trans_out_ref, out_ref,
    stream, normed, gate, keep, left, right,
    w_out, w_in, y_out, y_in, yb_out, yb_in, wb_out, wb_in,
    ready, root_ready, zs, zr, xs, xr,
):
    nz, nx, ti, tk = dims
    nc = CORES
    np_ = nc * nx
    tile, chan = pair_ref.shape
    hidden = tri_out_ref.shape[1]
    ffn = trans_out_ref.shape[0]
    size = nx * tk
    z, c, x = lax.axis_index("row_0"), lax.axis_index("row_1"), lax.axis_index("col")
    me = c * nx + x
    step, ti_step = tile // PIECES, ti // PIECES
    pieces = [slice(k * step, (k + 1) * step) for k in range(PIECES)]
    whole = slice(0, tile)
    lz, lp = log2(nz), log2(np_)
    far_first = sorted(range(1, nz), key=lambda d: -min(d, nz - d))
    others = [(dc, dx) for dx in sorted(range(nx), key=lambda d: -min(d, nx - d)) for dc in range(nc) if dc or dx]

    def z_peer(d):
        return lax.rem(z + d, nz)

    def x_peer(o):
        return lax.rem(c + o[0], nc), lax.rem(x + o[1], nx)

    first_column = ((c == 0) & (x == 0)).astype(jnp.int32)
    place = lax.rem(z - first_column + nz, nz)
    last_comer = (z == 0) & (first_column == 1)
    barrier = pltpu.get_barrier_semaphore()

    def at_z(t):
        return {"row_0": t}

    def at_x(o):
        tc, tx = x_peer(o)
        return {"row_1": tc, "col": tx}

    @pl.when(jnp.logical_not(last_comer))
    def _():
        for o in others:
            pl.semaphore_signal(barrier, inc=1, device_id=at_x(o), device_id_type=MESH)

    greeted = len(others) - ((z == 0) & jnp.logical_not(last_comer)).astype(jnp.int32) + (place > 0).astype(jnp.int32)

    def enter():
        pl.semaphore_wait(barrier, greeted)

        @pl.when(place < nz - 1)
        def _():
            pl.semaphore_signal(barrier, inc=1, device_id=at_z(z_peer(1)), device_id_type=MESH)

        for d in range(1, nz):

            @pl.when(place >= d)
            def _():
                pl.semaphore_signal(ready.at[place], inc=1, device_id=at_z(z_peer(nz - d)), device_id_type=MESH)

        @pl.when(last_comer)
        def _():
            for o in others:
                pl.semaphore_signal(root_ready, inc=1, device_id=at_x(o), device_id_type=MESH)

    def all_entered():
        @pl.when((z == 0) & jnp.logical_not(last_comer))
        def _():
            pl.semaphore_wait(root_ready, 1)

    started = []
    used = {"z": 0, "x": 0}

    def bank_of(kind):
        used[kind] += 1
        return used[kind] - 1

    def all_bytes(ref, count, rows, lanes, sem):
        blocks = ref.at[0:count, rows, lanes]
        return pltpu.make_async_copy(blocks, blocks, sem)

    def z_copy(source, target, rows, lanes, bank, t):
        return pltpu.make_async_remote_copy(
            src_ref=source.at[t, rows, lanes], dst_ref=target.at[z, rows, lanes],
            send_sem=zs.at[bank], recv_sem=zr.at[bank], device_id=at_z(t), device_id_type=MESH,
        )

    def z_send(source, target, rows, lanes):
        bank = bank_of("z")
        for d in far_first:
            z_copy(source, target, rows, lanes, bank, z_peer(d)).start()
        target[z, rows, lanes] = source[z, rows, lanes]
        started.append(all_bytes(source, nz - 1, rows, lanes, zs.at[bank]))
        return all_bytes(target, nz - 1, rows, lanes, zr.at[bank])

    def z_send_as_they_enter(source, target, rows, lanes):
        bank = bank_of("z")
        for q in range(nz):

            @pl.when(q > place)
            def _():
                pl.semaphore_wait(ready.at[q], 1)

            @pl.when(q != place)
            def _():
                z_copy(source, target, rows, lanes, bank, lax.rem(q + first_column, nz)).start()

        target[z, rows, lanes] = source[z, rows, lanes]
        started.append(all_bytes(source, nz - 1, rows, lanes, zs.at[bank]))
        return all_bytes(target, nz - 1, rows, lanes, zr.at[bank])

    def x_send(source, target, rows, lanes):
        bank = bank_of("x")
        for o in others:
            tc, tx = x_peer(o)
            pltpu.make_async_remote_copy(
                src_ref=source.at[tc * nx + tx, rows, lanes], dst_ref=target.at[me, rows, lanes],
                send_sem=xs.at[bank], recv_sem=xr.at[bank], device_id=at_x(o), device_id_type=MESH,
            ).start()
        target[me, rows, lanes] = source[me, rows, lanes]
        started.append(all_bytes(source, np_ - 1, rows, lanes, xs.at[bank]))
        return all_bytes(target, np_ - 1, rows, lanes, xr.at[bank])

    def arrive(copies):
        copies.wait()

    token = lax.broadcasted_iota(jnp.int32, (1, tile), 1)
    row = sum((token >= k * tk).astype(jnp.int32) for k in range(1, ti))
    limit = count_ref[0]
    inside = ((z * nc + c) * ti + row < limit) & (x * tk + token - row * tk < limit)
    keep[...] = jnp.where(inside, 1.0, 0.0).astype(F32)

    def project(side, lanes, which):
        v = normed[:, lanes]
        cols = slice(which * hidden, (which + 1) * hidden)
        gates = slice((2 + which) * hidden, (3 + which) * hidden)
        value = dot(tri_in_ref[side, :, cols], v, 0, 0)
        opening = dot(tri_in_ref[side, :, gates], v, 0, 0)
        return (keep[:, lanes] * jax.nn.sigmoid(opening) * value).astype(BF16)

    def set_gate(side, lanes):
        gate[:, lanes] = jax.nn.sigmoid(dot(tri_gate_ref[side], normed[:, lanes], 0, 0))

    def update_stream(side, lanes):
        got = wb_in[side, :, :, lanes].reshape(hidden, step)
        v = layer_norm(got.astype(F32)).astype(BF16)
        update = gate[:, lanes] * dot(tri_out_ref[side], v, 0, 0)
        return (stream[:, lanes].astype(F32) + keep[:, lanes] * update).astype(BF16)

    to_x = one_hot((hidden, hidden), lambda r: (r & (nz - 1)) * np_ + (r >> lz))
    to_z = one_hot((hidden, hidden), lambda r: (r & (np_ - 1)) * nz + (r >> lp))
    order = one_hot((size, size), lambda r: (r & (nz - 1)) * (nc * ti) + (r >> lz))

    def z_to_x(side, which, lanes):
        got = w_in[side, :, which * np_ : (which + 1) * np_, lanes]
        got = got.reshape(hidden, got.shape[2])
        y_out[side, :, which * nz : (which + 1) * nz, lanes] = dot(to_x, got, 1, 0).astype(BF16).reshape(np_, nz, got.shape[1])

    def x_to_z(side, lanes):
        got = yb_in[side, :, :, lanes].reshape(hidden, step)
        wb_out[side, :, :, lanes] = dot(to_z, got, 1, 0).astype(BF16).reshape(nz, np_, step)

    def gather_rows(source, target, rows_of, first):
        for cc in range(nc):
            for i in rows_of:
                base = (cc * len(rows_of) + i - rows_of[0]) * nz
                for xx in range(nx):
                    target[base : base + nz, xx * tk : (xx + 1) * tk] = source[
                        cc * nx + xx, first : first + nz, i * tk : (i + 1) * tk
                    ]

    def spread_rows(value, target, rows_of, row_first, row_count):
        for cc in range(nc):
            for i in rows_of:
                base = (cc * row_count + i - row_first) * nz
                for xx in range(nx):
                    target[cc * nx + xx, :, i * tk : (i + 1) * tk] = value[base : base + nz, xx * tk : (xx + 1) * tk]

    rows_of = [list(range(k * ti_step, (k + 1) * ti_step)) for k in range(PIECES)]
    rows_all = list(range(ti))

    both, a_rows, b_rows = slice(0, 2 * np_), slice(0, nz), slice(nz, 2 * nz)

    def project_both(side, lanes):
        w_out[side, :, 0:np_, lanes] = project(side, lanes, 0).reshape(nz, np_, step)
        w_out[side, :, np_ : 2 * np_, lanes] = project(side, lanes, 1).reshape(nz, np_, step)

    def go_back(side, k, arrivals):
        arrive(arrivals)
        x_to_z(side, pieces[k])
        return z_send(wb_out.at[side], wb_in.at[side], slice(0, np_), pieces[k])

    for lanes in pieces:
        v = pair_ref[lanes, :].astype(F32).T
        stream[:, lanes] = v.astype(BF16)
        normed[:, lanes] = layer_norm(v).astype(BF16)
        project_both(0, lanes)
        set_gate(0, lanes)
    enter()
    here = z_send_as_they_enter(w_out.at[0], w_in.at[0], both, whole)
    all_entered()
    arrive(here)
    for lanes in pieces:
        z_to_x(0, 1, lanes)
    b_there = x_send(y_out.at[0], y_in.at[0], b_rows, whole)
    there = []
    for lanes in pieces:
        z_to_x(0, 0, lanes)
        there.append(x_send(y_out.at[0], y_in.at[0], a_rows, lanes))
    arrive(b_there)
    gather_rows(y_in.at[0], right, rows_all, nz)

    def multiply(k):
        arrive(there[k])
        gather_rows(y_in.at[0], left.at[k], rows_of[k], 0)
        product = dot(left[k], right[...], 1, 1).astype(BF16)
        value = dot(product, order, 1, 0).astype(BF16)
        spread_rows(value, yb_out.at[0], rows_of[k], rows_of[k][0], ti_step)
        return x_send(yb_out.at[0], yb_in.at[0], a_rows, pieces[k])

    mixed, home = [multiply(0)], []
    for k in range(PIECES):
        if k + 1 < PIECES:
            mixed.append(multiply(k + 1))
        home.append(go_back(0, k, mixed[k]))

    here = []
    for k, lanes in enumerate(pieces):
        arrive(home[k])
        v = update_stream(0, lanes)
        stream[:, lanes] = v
        normed[:, lanes] = layer_norm(v.astype(F32)).astype(BF16)
        project_both(1, lanes)
        here.append(z_send(w_out.at[1], w_in.at[1], both, lanes))
        set_gate(1, lanes)

    def forward(k):
        arrive(here[k])
        z_to_x(1, 0, pieces[k])
        z_to_x(1, 1, pieces[k])
        return x_send(y_out.at[1], y_in.at[1], slice(0, 2 * nz), pieces[k])

    count = ti_step * nc * nz

    def add(k, arrivals, so_far):
        arrive(arrivals)
        gather_rows(y_in.at[1], left.at[k], rows_of[k], 0)
        gather_rows(y_in.at[1], right.at[k * count : (k + 1) * count], rows_of[k], nz)
        turned = dot(order, left[k], 1, 1).astype(BF16)
        part = dot(turned, right[k * count : (k + 1) * count], 1, 0)
        return part if so_far is None else so_far + part

    there, sum_ = [forward(0)], None
    for k in range(PIECES):
        if k + 1 < PIECES:
            there.append(forward(k + 1))
        sum_ = add(k, there[k], sum_)
    value = sum_.astype(BF16)
    mixed = []
    for k in range(PIECES):
        spread_rows(value, yb_out.at[1], rows_of[k], 0, ti)
        mixed.append(x_send(yb_out.at[1], yb_in.at[1], a_rows, pieces[k]))
    home = [go_back(1, k, mixed[k]) for k in range(PIECES)]

    for k, lanes in enumerate(pieces):
        arrive(home[k])
        base = update_stream(1, lanes).astype(F32)
        v = layer_norm(base).astype(BF16)
        inner = dot(trans_in_ref[...], v, 0, 0)
        act = (jax.nn.silu(inner[:ffn]) * inner[ffn:]).astype(BF16)
        update = dot(trans_out_ref[...], act, 0, 0)
        out_ref[lanes, :] = (base + keep[:, lanes] * update).T.astype(BF16)

    for copies in started:
        copies.wait()


def body(pair, token_count, tri_in, tri_gate, tri_out, trans_in, trans_out):
    ti, tk, chan = pair.shape
    hidden = tri_out.shape[1]
    nz, nx = lax.axis_size("row_0"), lax.axis_size("col")
    np_ = CORES * nx
    tile, size = ti * tk, nx * tk
    vmem = pl.BlockSpec(memory_space=pltpu.VMEM)
    sem = pltpu.SemaphoreType.DMA

    def buffers(*shape):
        return [pltpu.VMEM(shape, BF16)] * 2

    z_banks, x_banks = 1 + 3 * PIECES, 1 + 4 * PIECES
    out = pl.pallas_call(
        functools.partial(kernel, (nz, nx, ti, tk)),
        out_shape=jax.ShapeDtypeStruct((tile, chan), BF16),
        in_specs=[pl.BlockSpec(memory_space=pltpu.SMEM)] + [vmem] * 6,
        out_specs=vmem,
        scratch_shapes=[
            pltpu.VMEM((chan, tile), BF16),
            pltpu.VMEM((chan, tile), BF16),
            pltpu.VMEM((chan, tile), F32),
            pltpu.VMEM((1, tile), F32),
            pltpu.VMEM((PIECES, size // PIECES, size), BF16),
            pltpu.VMEM((size, size), BF16),
            *buffers(2, nz, 2 * np_, tile),
            *buffers(2, np_, 2 * nz, tile),
            *buffers(2, np_, nz, tile),
            *buffers(2, nz, np_, tile),
            pltpu.SemaphoreType.REGULAR((nz,)), pltpu.SemaphoreType.REGULAR,
            sem((z_banks,)), sem((z_banks,)), sem((x_banks,)), sem((x_banks,)),
        ],
        compiler_params=pltpu.CompilerParams(
            collective_id=0, has_side_effects=True, vmem_limit_bytes=56 * 1024 * 1024
        ),
        name="pairformer_block",
    )(token_count, pair.reshape(tile, chan), tri_in, tri_gate, tri_out, trans_in, trans_out)
    return out.reshape(ti, tk, chan)


def solution(mesh):
    torus = Mesh(
        mesh.devices.reshape(mesh.shape["grp"], mesh.shape["row"] // CORES, CORES, mesh.shape["col"]),
        ("grp", "row_0", "row_1", "col"),
    )
    grp_row = ("grp", "row_0", "row_1")
    placed = (P(grp_row, "col", None), P("grp"), P(), P(), P(), P(), P())
    return jax.shard_map(
        body, mesh=torus, in_specs=placed, out_specs=P(grp_row, "col", None), check_vma=False
    )
```

profile of v0, /device:TPU:33, one launch (start us, length us, event | category | flops | bytes accessed | tf_op | source)
XLA Modules:
  0.0 135.4 jit_solution(9117166184017840351)
XLA Ops:
  0.7 133.0 %pairformer_block.1 = bf16[1152,128]{1,0:T(8,128)(2,1)} custom-call(s32[1]{0:T(128)S(6)} %copy.9.count_ref, bf16[1152,128]{1,0:T(8,128)(2,1)} %bitcast.3, bf16[2,128,512]{2,1,0:T(8,128)(2,1)} %tri_in_ref.1, bf16[2,128,128]{2,1,0:T(8,128)(2,1)} %tri_gate_ref.1, bf16[2,128,128]{2,1,0:T(8,128)(2,1)} %tri_out_ref.1, bf16[128,1024]{1,0:T(8,128)(2,1)} %trans_in_ref.1, ...), custom_call_target="tpu_custom_call" | custom-call | tf_op jit(solution)/shard_map/pairformer_block/pallas_call | solution.py:329
  133.7 1.7 %copy.10 = bf16[12,96,128]{2,1,0:T(8,128)(2,1)} copy(bf16[12,96,128]{2,1,0:T(8,128)(2,1)} %bitcast.2) | data formatting | bytes 589824
where the time goes:
time: 136 us; the launch traced here: 135 us
  Pallas kernels  133 us (98%)
  local copies, waits for them, and re-layouts  1.69 us (1%)
    pallas_call x1, Pallas kernels, body(): pl.pallas_call(functools.partial(kernel, (nz, nx, ti, tk)), out_shape=jax...  133 us

commit v1 on v0

v1 whole, which is shorter than its diff:
```python
import functools

import jax
import jax.numpy as jnp
from jax import lax
from jax.experimental import pallas as pl
from jax.experimental.pallas import tpu as pltpu
from jax.sharding import Mesh
from jax.sharding import PartitionSpec as P

MESH = pl.DeviceIdType.MESH
F32, BF16 = jnp.float32, jnp.bfloat16
CORES = 2
PIECES = 3


def log2(n):
    assert n & (n - 1) == 0
    return n.bit_length() - 1


def dot(a, b, ca, cb):
    return lax.dot_general(a, b, (((ca,), (cb,)), ((), ())), preferred_element_type=F32)


def layer_norm(v):
    average = jnp.mean(v, axis=0, keepdims=True)
    centred = v - average
    spread = jnp.mean(centred * centred, axis=0, keepdims=True)
    return centred * lax.rsqrt(spread + 1e-05)


def one_hot(shape, source_of_row):
    row = lax.broadcasted_iota(jnp.int32, shape, 0)
    col = lax.broadcasted_iota(jnp.int32, shape, 1)
    return (source_of_row(row) == col).astype(F32).astype(BF16)


def kernel(
    dims, count_ref, pair_ref, tri_in_ref, tri_gate_ref, tri_out_ref, trans_in_ref, trans_out_ref, out_ref,
    stream, stream_c, normed, normed_c, gate, keep, left, right, turned, right_c,
    w_out, w_in, y_out, y_in, yb_out, yb_in, wb_out, wb_in,
    zs, zr, xs, xr,
):
    nz, nx, ti, tk = dims
    nc = CORES
    np_ = nc * nx
    tile, chan = pair_ref.shape
    hidden = tri_out_ref.shape[1]
    ffn = trans_out_ref.shape[0]
    size = nx * tk
    z, c, x = lax.axis_index("row_0"), lax.axis_index("row_1"), lax.axis_index("col")
    me = c * nx + x
    step, ti_step, part = tile // PIECES, ti // PIECES, tk // PIECES
    count = ti_step * nc * nz
    pieces = [slice(k * step, (k + 1) * step) for k in range(PIECES)]
    whole = slice(0, tile)
    lz, lp = log2(nz), log2(np_)
    far_first = sorted(range(1, nz), key=lambda d: -min(d, nz - d))
    others = [(dc, dx) for dx in sorted(range(nx), key=lambda d: -min(d, nx - d)) for dc in range(nc) if dc or dx]

    def z_peer(d):
        return lax.rem(z + d, nz)

    def x_peer(o):
        return lax.rem(c + o[0], nc), lax.rem(x + o[1], nx)

    def at_z(t):
        return {"row_0": t}

    def at_x(o):
        tc, tx = x_peer(o)
        return {"row_1": tc, "col": tx}

    barrier = pltpu.get_barrier_semaphore()
    for d in far_first:
        pl.semaphore_signal(barrier, inc=1, device_id=at_z(z_peer(d)), device_id_type=MESH)
    for o in others:
        pl.semaphore_signal(barrier, inc=1, device_id=at_x(o), device_id_type=MESH)

    started = []
    used = {"z": 0, "x": 0}

    def bank_of(kind):
        used[kind] += 1
        return used[kind] - 1

    def all_bytes(ref, count, rows, lanes, sem):
        blocks = ref.at[0:count, rows, lanes]
        return pltpu.make_async_copy(blocks, blocks, sem)

    def z_copy(source, target, rows, lanes, bank, t):
        return pltpu.make_async_remote_copy(
            src_ref=source.at[t, rows, lanes], dst_ref=target.at[z, rows, lanes],
            send_sem=zs.at[bank], recv_sem=zr.at[bank], device_id=at_z(t), device_id_type=MESH,
        )

    def z_send(source, target, rows, lanes):
        bank = bank_of("z")
        for d in far_first:
            z_copy(source, target, rows, lanes, bank, z_peer(d)).start()
        target[z, rows, lanes] = source[z, rows, lanes]
        started.append(all_bytes(source, nz - 1, rows, lanes, zs.at[bank]))
        return all_bytes(target, nz - 1, rows, lanes, zr.at[bank])

    def x_send(source, target, rows, lanes):
        bank = bank_of("x")
        for o in others:
            tc, tx = x_peer(o)
            pltpu.make_async_remote_copy(
                src_ref=source.at[tc * nx + tx, rows, lanes], dst_ref=target.at[me, rows, lanes],
                send_sem=xs.at[bank], recv_sem=xr.at[bank], device_id=at_x(o), device_id_type=MESH,
            ).start()
        target[me, rows, lanes] = source[me, rows, lanes]
        started.append(all_bytes(source, np_ - 1, rows, lanes, xs.at[bank]))
        return all_bytes(target, np_ - 1, rows, lanes, xr.at[bank])

    def arrive(copies):
        copies.wait()

    token = lax.broadcasted_iota(jnp.int32, (1, tile), 1)
    limit = count_ref[0]

    def inside(row, col):
        valid = ((z * nc + c) * ti + row < limit) & (x * tk + col < limit)
        return jnp.where(valid, 1.0, 0.0).astype(F32)

    def count_steps(value, length, most):
        return sum((value >= m * length).astype(jnp.int32) for m in range(1, most))

    by_row = count_steps(token, tk, ti)
    keep[0:1] = inside(by_row, token - by_row * tk)
    piece = count_steps(token, step, PIECES)
    rest = token - piece * step
    by_row = count_steps(rest, part, ti)
    keep[1:2] = inside(by_row, piece * part + rest - by_row * part)

    def by_columns(source, target, rows_of_piece):
        for i in rows_of_piece:
            for q in range(PIECES):
                at = q * step + i * part
                target[:, at : at + part] = source[:, i * tk + q * part : i * tk + (q + 1) * part]

    def project(side, lanes, which, source, mask):
        v = source[:, lanes]
        cols = slice(which * hidden, (which + 1) * hidden)
        gates = slice((2 + which) * hidden, (3 + which) * hidden)
        value = dot(tri_in_ref[side, :, cols], v, 0, 0)
        opening = dot(tri_in_ref[side, :, gates], v, 0, 0)
        value = (keep[mask : mask + 1, lanes] * jax.nn.sigmoid(opening) * value).astype(BF16)
        w_out[side, :, which * np_ : (which + 1) * np_, lanes] = value.reshape(nz, np_, step)

    def set_gate(side, lanes, source):
        gate[:, lanes] = jax.nn.sigmoid(dot(tri_gate_ref[side], source[:, lanes], 0, 0))

    def update_stream(side, lanes, source):
        got = wb_in[side, :, :, lanes].reshape(hidden, step)
        v = layer_norm(got.astype(F32)).astype(BF16)
        update = gate[:, lanes] * dot(tri_out_ref[side], v, 0, 0)
        return (source[:, lanes].astype(F32) + keep[side : side + 1, lanes] * update).astype(BF16)

    to_x = one_hot((hidden, hidden), lambda r: (r & (nz - 1)) * np_ + (r >> lz))
    to_z = one_hot((hidden, hidden), lambda r: (r & (np_ - 1)) * nz + (r >> lp))
    order = one_hot((size, size), lambda r: (r & (nz - 1)) * (nc * ti) + (r >> lz))

    def z_to_x(side, which, lanes):
        got = w_in[side, :, which * np_ : (which + 1) * np_, lanes]
        got = got.reshape(hidden, got.shape[2])
        y_out[side, :, which * nz : (which + 1) * nz, lanes] = dot(to_x, got, 1, 0).astype(BF16).reshape(np_, nz, got.shape[1])

    def x_to_z(side, lanes):
        got = yb_in[side, :, :, lanes].reshape(hidden, step)
        wb_out[side, :, :, lanes] = dot(to_z, got, 1, 0).astype(BF16).reshape(nz, np_, step)

    def gather_rows(source, target, rows_of, rows, lane, width):
        for cc in range(nc):
            for i in rows_of:
                base = (cc * len(rows_of) + i - rows_of[0]) * nz
                at = lane + i * width
                for xx in range(nx):
                    target[base : base + nz, xx * width : (xx + 1) * width] = source[cc * nx + xx, rows, at : at + width]

    def spread_rows(value, target, rows_of, lane, width):
        for cc in range(nc):
            for i in rows_of:
                base = (cc * len(rows_of) + i - rows_of[0]) * nz
                at = lane + i * width
                for xx in range(nx):
                    target[cc * nx + xx, :, at : at + width] = value[base : base + nz, xx * width : (xx + 1) * width]

    rows_of = [list(range(k * ti_step, (k + 1) * ti_step)) for k in range(PIECES)]
    rows_all = list(range(ti))

    a_in, b_in = slice(0, np_), slice(np_, 2 * np_)
    a_rows, b_rows = slice(0, nz), slice(nz, 2 * nz)

    def send_w(side, rows, lanes):
        return z_send(w_out.at[side], w_in.at[side], rows, lanes)

    def forward(side, which, lanes, arrivals):
        arrive(arrivals)
        z_to_x(side, which, lanes)
        return x_send(y_out.at[side], y_in.at[side], (a_rows, b_rows)[which], lanes)

    def go_back(side, k, arrivals):
        arrive(arrivals)
        x_to_z(side, pieces[k])
        return z_send(wb_out.at[side], wb_in.at[side], slice(0, np_), pieces[k])

    for lanes in pieces:
        v = pair_ref[lanes, :].astype(F32).T
        stream[:, lanes] = v.astype(BF16)
        normed[:, lanes] = layer_norm(v).astype(BF16)
        project(0, lanes, 1, normed, 0)
    for lanes in pieces:
        project(0, lanes, 0, normed, 0)
    pl.semaphore_wait(barrier, len(far_first) + len(others))
    b_here = send_w(0, b_in, whole)
    a_here = [send_w(0, a_in, lanes) for lanes in pieces]
    for lanes in pieces:
        set_gate(0, lanes, normed)
    arrive(b_here)
    for lanes in pieces:
        z_to_x(0, 1, lanes)
    b_there = x_send(y_out.at[0], y_in.at[0], b_rows, whole)
    there = [forward(0, 0, pieces[0], a_here[0])]
    arrive(b_there)
    gather_rows(y_in.at[0], right, rows_all, b_rows, 0, tk)

    def multiply(k):
        arrive(there[k])
        gather_rows(y_in.at[0], left.at[k * count : (k + 1) * count], rows_of[k], a_rows, 0, tk)
        product = dot(left[k * count : (k + 1) * count], right[...], 1, 1).astype(BF16)
        value = dot(product, order, 1, 0).astype(BF16)
        spread_rows(value, yb_out.at[0], rows_of[k], 0, tk)
        return x_send(yb_out.at[0], yb_in.at[0], a_rows, pieces[k])

    mixed, home = [], []
    for k in range(PIECES):
        mixed.append(multiply(k))
        if k + 1 < PIECES:
            there.append(forward(0, 0, pieces[k + 1], a_here[k + 1]))
        if k > 0:
            home.append(go_back(0, k - 1, mixed[k - 1]))
    home.append(go_back(0, PIECES - 1, mixed[PIECES - 1]))

    a_here = []
    for k, lanes in enumerate(pieces):
        arrive(home[k])
        v = update_stream(0, lanes, stream)
        stream[:, lanes] = v
        normed[:, lanes] = layer_norm(v.astype(F32)).astype(BF16)
        project(1, lanes, 0, normed, 0)
        a_here.append(send_w(1, a_in, lanes))
        by_columns(normed, normed_c, rows_of[k])
    b_here = []
    for lanes in pieces:
        project(1, lanes, 1, normed_c, 1)
        b_here.append(send_w(1, b_in, lanes))
    by_columns(stream, stream_c, rows_all)
    for lanes in pieces:
        set_gate(1, lanes, normed_c)
    there = [forward(1, 0, pieces[k], a_here[k]) for k in range(PIECES)]
    for k in range(PIECES):
        arrive(there[k])
        gather_rows(y_in.at[1], left.at[k * count : (k + 1) * count], rows_of[k], a_rows, 0, tk)
        turned[:, k * count : (k + 1) * count] = dot(order, left[k * count : (k + 1) * count], 1, 1).astype(BF16)
    there = [forward(1, 1, pieces[0], b_here[0])]

    def multiply(q):
        arrive(there[q])
        for k in range(PIECES):
            gather_rows(y_in.at[1], right_c.at[q, k * count : (k + 1) * count], rows_of[k], b_rows, q * step, part)
        value = dot(turned[...], right_c[q], 1, 0).astype(BF16)
        spread_rows(value, yb_out.at[1], rows_all, q * step, part)
        return x_send(yb_out.at[1], yb_in.at[1], a_rows, pieces[q])

    mixed, home = [], []
    for q in range(PIECES):
        mixed.append(multiply(q))
        if q + 1 < PIECES:
            there.append(forward(1, 1, pieces[q + 1], b_here[q + 1]))
        if q > 0:
            home.append(go_back(1, q - 1, mixed[q - 1]))
    home.append(go_back(1, PIECES - 1, mixed[PIECES - 1]))

    for q, lanes in enumerate(pieces):
        arrive(home[q])
        base = update_stream(1, lanes, stream_c).astype(F32)
        v = layer_norm(base).astype(BF16)
        inner = dot(trans_in_ref[...], v, 0, 0)
        act = (jax.nn.silu(inner[:ffn]) * inner[ffn:]).astype(BF16)
        update = dot(trans_out_ref[...], act, 0, 0)
        result = (base + keep[1:2, lanes] * update).T.astype(BF16)
        for i in range(ti):
            out_ref[i * tk + q * part : i * tk + (q + 1) * part, :] = result[i * part : (i + 1) * part]

    for copies in started:
        copies.wait()


def body(pair, token_count, tri_in, tri_gate, tri_out, trans_in, trans_out):
    ti, tk, chan = pair.shape
    hidden = tri_out.shape[1]
    nz, nx = lax.axis_size("row_0"), lax.axis_size("col")
    np_ = CORES * nx
    tile, size = ti * tk, nx * tk
    vmem = pl.BlockSpec(memory_space=pltpu.VMEM)
    sem = pltpu.SemaphoreType.DMA

    def buffers(*shape):
        return [pltpu.VMEM(shape, BF16)] * 2

    z_banks, x_banks = 1 + 5 * PIECES, 1 + 5 * PIECES
    out = pl.pallas_call(
        functools.partial(kernel, (nz, nx, ti, tk)),
        out_shape=jax.ShapeDtypeStruct((tile, chan), BF16),
        in_specs=[pl.BlockSpec(memory_space=pltpu.SMEM)] + [vmem] * 6,
        out_specs=vmem,
        scratch_shapes=[
            *buffers(chan, tile),
            *buffers(chan, tile),
            pltpu.VMEM((chan, tile), F32),
            pltpu.VMEM((2, tile), F32),
            *buffers(size, size),
            pltpu.VMEM((size, size), BF16),
            pltpu.VMEM((PIECES, size, size // PIECES), BF16),
            *buffers(2, nz, 2 * np_, tile),
            *buffers(2, np_, 2 * nz, tile),
            *buffers(2, np_, nz, tile),
            *buffers(2, nz, np_, tile),
            sem((z_banks,)), sem((z_banks,)), sem((x_banks,)), sem((x_banks,)),
        ],
        compiler_params=pltpu.CompilerParams(
            collective_id=0, has_side_effects=True, vmem_limit_bytes=56 * 1024 * 1024
        ),
        name="pairformer_block",
    )(token_count, pair.reshape(tile, chan), tri_in, tri_gate, tri_out, trans_in, trans_out)
    return out.reshape(ti, tk, chan)


def solution(mesh):
    torus = Mesh(
        mesh.devices.reshape(mesh.shape["grp"], mesh.shape["row"] // CORES, CORES, mesh.shape["col"]),
        ("grp", "row_0", "row_1", "col"),
    )
    grp_row = ("grp", "row_0", "row_1")
    placed = (P(grp_row, "col", None), P("grp"), P(), P(), P(), P(), P())
    return jax.shard_map(
        body, mesh=torus, in_specs=placed, out_specs=P(grp_row, "col", None), check_vma=False
    )
```

time: 136 us -> 126 us (0.926)
  Pallas kernels: 133 us -> 123 us
    pallas_call x1, Pallas kernels: 133 us -> 123 us  [body(): pl.pallas_call(functools.partial(kernel, (nz, nx, ti, tk)), out_shape=jax...]
where the time goes in v1:
time: 126 us; the launch traced here: 125 us
  Pallas kernels  123 us (98%)
  local copies, waits for them, and re-layouts  1.69 us (1%)
    pallas_call x1, Pallas kernels, body(): pl.pallas_call(functools.partial(kernel, (nz, nx, ti, tk)), out_shape=jax...  123 us

profile of v1, /device:TPU:33, one launch (start us, length us, event | category | flops | bytes accessed | tf_op | source)
XLA Modules:
  0.0 125.5 jit_solution(15597421418158815175)
XLA Ops:
  0.7 123.1 %pairformer_block.1 = bf16[1152,128]{1,0:T(8,128)(2,1)} custom-call(s32[1]{0:T(128)S(6)} %copy.9.count_ref, bf16[1152,128]{1,0:T(8,128)(2,1)} %bitcast.3, bf16[2,128,512]{2,1,0:T(8,128)(2,1)} %tri_in_ref.1, bf16[2,128,128]{2,1,0:T(8,128)(2,1)} %tri_gate_ref.1, bf16[2,128,128]{2,1,0:T(8,128)(2,1)} %tri_out_ref.1, bf16[128,1024]{1,0:T(8,128)(2,1)} %trans_in_ref.1, ...), custom_call_target="tpu_custom_call" | custom-call | tf_op jit(solution)/shard_map/pairformer_block/pallas_call | solution.py:315
  123.8 1.7 %copy.10 = bf16[12,96,128]{2,1,0:T(8,128)(2,1)} copy(bf16[12,96,128]{2,1,0:T(8,128)(2,1)} %bitcast.2) | data formatting | bytes 589824

commit v2 on v1

--- a/solution.py
+++ b/solution.py
@@ -207,42 +207,52 @@
         x_to_z(side, pieces[k])
         return z_send(wb_out.at[side], wb_in.at[side], slice(0, np_), pieces[k])
 
-    for lanes in pieces:
+    def in_steps(forth, product, back, first):
+        there, mixed, home = {0: first}, {}, {}
+        there[1] = forth(1)
+        for k in range(PIECES):
+            mixed[k] = product(k, there[k])
+            if k + 2 < PIECES:
+                there[k + 2] = forth(k + 2)
+            if k > 0:
+                home[k - 1] = back(k - 1, mixed[k - 1])
+        home[PIECES - 1] = back(PIECES - 1, mixed[PIECES - 1])
+        return [home[k] for k in range(PIECES)]
+
+    b_here, a_here = [], []
+    for k, lanes in enumerate(pieces):
         v = pair_ref[lanes, :].astype(F32).T
         stream[:, lanes] = v.astype(BF16)
         normed[:, lanes] = layer_norm(v).astype(BF16)
         project(0, lanes, 1, normed, 0)
+        if k == 0:
+            pl.semaphore_wait(barrier, len(far_first) + len(others))
+        b_here.append(send_w(0, b_in, lanes))
     for lanes in pieces:
         project(0, lanes, 0, normed, 0)
-    pl.semaphore_wait(barrier, len(far_first) + len(others))
-    b_here = send_w(0, b_in, whole)
-    a_here = [send_w(0, a_in, lanes) for lanes in pieces]
+        a_here.append(send_w(0, a_in, lanes))
     for lanes in pieces:
         set_gate(0, lanes, normed)
-    arrive(b_here)
-    for lanes in pieces:
+    for lanes, arrivals in zip(pieces, b_here):
+        arrive(arrivals)
         z_to_x(0, 1, lanes)
     b_there = x_send(y_out.at[0], y_in.at[0], b_rows, whole)
     there = [forward(0, 0, pieces[0], a_here[0])]
     arrive(b_there)
     gather_rows(y_in.at[0], right, rows_all, b_rows, 0, tk)
 
-    def multiply(k):
-        arrive(there[k])
+    def multiply(k, arrivals):
+        arrive(arrivals)
         gather_rows(y_in.at[0], left.at[k * count : (k + 1) * count], rows_of[k], a_rows, 0, tk)
         product = dot(left[k * count : (k + 1) * count], right[...], 1, 1).astype(BF16)
         value = dot(product, order, 1, 0).astype(BF16)
         spread_rows(value, yb_out.at[0], rows_of[k], 0, tk)
         return x_send(yb_out.at[0], yb_in.at[0], a_rows, pieces[k])
 
-    mixed, home = [], []
-    for k in range(PIECES):
-        mixed.append(multiply(k))
-        if k + 1 < PIECES:
-            there.append(forward(0, 0, pieces[k + 1], a_here[k + 1]))
-        if k > 0:
-            home.append(go_back(0, k - 1, mixed[k - 1]))
-    home.append(go_back(0, PIECES - 1, mixed[PIECES - 1]))
+    def forward_a(k):
+        return forward(0, 0, pieces[k], a_here[k])
+
+    home = in_steps(forward_a, multiply, lambda k, arrivals: go_back(0, k, arrivals), there[0])
 
     a_here = []
     for k, lanes in enumerate(pieces):
@@ -267,22 +277,18 @@
         turned[:, k * count : (k + 1) * count] = dot(order, left[k * count : (k + 1) * count], 1, 1).astype(BF16)
     there = [forward(1, 1, pieces[0], b_here[0])]
 
-    def multiply(q):
-        arrive(there[q])
+    def multiply(q, arrivals):
+        arrive(arrivals)
         for k in range(PIECES):
             gather_rows(y_in.at[1], right_c.at[q, k * count : (k + 1) * count], rows_of[k], b_rows, q * step, part)
         value = dot(turned[...], right_c[q], 1, 0).astype(BF16)
         spread_rows(value, yb_out.at[1], rows_all, q * step, part)
         return x_send(yb_out.at[1], yb_in.at[1], a_rows, pieces[q])
 
-    mixed, home = [], []
-    for q in range(PIECES):
-        mixed.append(multiply(q))
-        if q + 1 < PIECES:
-            there.append(forward(1, 1, pieces[q + 1], b_here[q + 1]))
-        if q > 0:
-            home.append(go_back(1, q - 1, mixed[q - 1]))
-    home.append(go_back(1, PIECES - 1, mixed[PIECES - 1]))
+    def forward_b(q):
+        return forward(1, 1, pieces[q], b_here[q])
+
+    home = in_steps(forward_b, multiply, lambda q, arrivals: go_back(1, q, arrivals), there[0])
 
     for q, lanes in enumerate(pieces):
         arrive(home[q])
@@ -311,7 +317,7 @@
     def buffers(*shape):
         return [pltpu.VMEM(shape, BF16)] * 2
 
-    z_banks, x_banks = 1 + 5 * PIECES, 1 + 5 * PIECES
+    z_banks, x_banks = 6 * PIECES, 1 + 5 * PIECES
     out = pl.pallas_call(
         functools.partial(kernel, (nz, nx, ti, tk)),
         out_shape=jax.ShapeDtypeStruct((tile, chan), BF16),

time: 126 us -> 122 us (0.968)
  Pallas kernels: 123 us -> 120 us
    pallas_call x1, Pallas kernels: 123 us -> 120 us  [body(): pl.pallas_call(functools.partial(kernel, (nz, nx, ti, tk)), out_shape=jax...]
where the time goes in v2:
time: 122 us
  Pallas kernels  120 us (98%)
  local copies, waits for them, and re-layouts  1.69 us (1%)
    pallas_call x1, Pallas kernels, body(): pl.pallas_call(functools.partial(kernel, (nz, nx, ti, tk)), out_shape=jax...  120 us

profile of v2, /device:TPU:33, one launch (start us, length us, event | category | flops | bytes accessed | tf_op | source)
XLA Modules:
  0.0 121.9 jit_solution(6602523362696491035)
XLA Ops:
  0.7 119.6 %pairformer_block.1 = bf16[1152,128]{1,0:T(8,128)(2,1)} custom-call(s32[1]{0:T(128)S(6)} %copy.9.count_ref, bf16[1152,128]{1,0:T(8,128)(2,1)} %bitcast.3, bf16[2,128,512]{2,1,0:T(8,128)(2,1)} %tri_in_ref.1, bf16[2,128,128]{2,1,0:T(8,128)(2,1)} %tri_gate_ref.1, bf16[2,128,128]{2,1,0:T(8,128)(2,1)} %tri_out_ref.1, bf16[128,1024]{1,0:T(8,128)(2,1)} %trans_in_ref.1, ...), custom_call_target="tpu_custom_call" | custom-call | tf_op jit(solution)/shard_map/pairformer_block/pallas_call | solution.py:321
  120.2 1.7 %copy.10 = bf16[12,96,128]{2,1,0:T(8,128)(2,1)} copy(bf16[12,96,128]{2,1,0:T(8,128)(2,1)} %bitcast.2) | data formatting | bytes 589824

commit v3 on v2

--- a/solution.py
+++ b/solution.py
@@ -39,7 +39,7 @@
 def kernel(
     dims, count_ref, pair_ref, tri_in_ref, tri_gate_ref, tri_out_ref, trans_in_ref, trans_out_ref, out_ref,
     stream, stream_c, normed, normed_c, gate, keep, left, right, turned, right_c,
-    w_out, w_in, y_out, y_in, yb_out, yb_in, wb_out, wb_in,
+    w_out, w_in, y_out, y_in, yb_out, yb_in, wb_out, wb_in, zc_out, zc_in,
     zs, zr, xs, xr,
 ):
     nz, nx, ti, tk = dims
@@ -153,24 +153,20 @@
     def set_gate(side, lanes, source):
         gate[:, lanes] = jax.nn.sigmoid(dot(tri_gate_ref[side], source[:, lanes], 0, 0))
 
-    def update_stream(side, lanes, source):
-        got = wb_in[side, :, :, lanes].reshape(hidden, step)
+    def update_stream(side, lanes, source, arrived, weights):
+        got = arrived[:, :, lanes].reshape(hidden, step)
         v = layer_norm(got.astype(F32)).astype(BF16)
-        update = gate[:, lanes] * dot(tri_out_ref[side], v, 0, 0)
+        update = gate[:, lanes] * dot(weights, v, 0, 0)
         return (source[:, lanes].astype(F32) + keep[side : side + 1, lanes] * update).astype(BF16)
-
-    to_x = one_hot((hidden, hidden), lambda r: (r & (nz - 1)) * np_ + (r >> lz))
-    to_z = one_hot((hidden, hidden), lambda r: (r & (np_ - 1)) * nz + (r >> lp))
-    order = one_hot((size, size), lambda r: (r & (nz - 1)) * (nc * ti) + (r >> lz))
 
     def z_to_x(side, which, lanes):
         got = w_in[side, :, which * np_ : (which + 1) * np_, lanes]
         got = got.reshape(hidden, got.shape[2])
         y_out[side, :, which * nz : (which + 1) * nz, lanes] = dot(to_x, got, 1, 0).astype(BF16).reshape(np_, nz, got.shape[1])
 
-    def x_to_z(side, lanes):
-        got = yb_in[side, :, :, lanes].reshape(hidden, step)
-        wb_out[side, :, :, lanes] = dot(to_z, got, 1, 0).astype(BF16).reshape(nz, np_, step)
+    def x_to_z(lanes):
+        got = yb_in[1, :, :, lanes].reshape(hidden, step)
+        wb_out[:, :, lanes] = dot(to_z, got, 1, 0).astype(BF16).reshape(nz, np_, step)
 
     def gather_rows(source, target, rows_of, rows, lane, width):
         for cc in range(nc):
@@ -202,10 +198,10 @@
         z_to_x(side, which, lanes)
         return x_send(y_out.at[side], y_in.at[side], (a_rows, b_rows)[which], lanes)
 
-    def go_back(side, k, arrivals):
-        arrive(arrivals)
-        x_to_z(side, pieces[k])
-        return z_send(wb_out.at[side], wb_in.at[side], slice(0, np_), pieces[k])
+    def go_back(k, arrivals):
+        arrive(arrivals)
+        x_to_z(pieces[k])
+        return z_send(wb_out, wb_in, a_in, pieces[k])
 
     def in_steps(forth, product, back, first):
         there, mixed, home = {0: first}, {}, {}
@@ -231,6 +227,13 @@
     for lanes in pieces:
         project(0, lanes, 0, normed, 0)
         a_here.append(send_w(0, a_in, lanes))
+    to_x = one_hot((hidden, hidden), lambda r: (r & (nz - 1)) * np_ + (r >> lz))
+    to_z = one_hot((hidden, hidden), lambda r: (r & (np_ - 1)) * nz + (r >> lp))
+    order = one_hot((size, size), lambda r: (r & (nz - 1)) * (nc * ti) + (r >> lz))
+    row_places = nc * ti_step
+    by_z = one_hot((count, count), lambda r: (r & (row_places - 1)) * nz + (r >> log2(row_places)))
+    by_row = one_hot((count, count), lambda r: (r & (nz - 1)) * row_places + (r >> lz))
+    out_weights = dot(to_x, tri_out_ref[0], 1, 0).astype(BF16)
     for lanes in pieces:
         set_gate(0, lanes, normed)
     for lanes, arrivals in zip(pieces, b_here):
@@ -246,18 +249,28 @@
         gather_rows(y_in.at[0], left.at[k * count : (k + 1) * count], rows_of[k], a_rows, 0, tk)
         product = dot(left[k * count : (k + 1) * count], right[...], 1, 1).astype(BF16)
         value = dot(product, order, 1, 0).astype(BF16)
+        zc_out[k] = dot(by_z, value, 1, 0).astype(BF16).reshape(nz, row_places, size)
+        return z_send(zc_out.at[k], zc_in.at[k], slice(0, row_places), slice(0, size))
+
+    def turn(k, arrivals):
+        arrive(arrivals)
+        value = dot(by_row, zc_in[k].reshape(count, size), 1, 0).astype(BF16)
         spread_rows(value, yb_out.at[0], rows_of[k], 0, tk)
         return x_send(yb_out.at[0], yb_in.at[0], a_rows, pieces[k])
 
-    def forward_a(k):
-        return forward(0, 0, pieces[k], a_here[k])
-
-    home = in_steps(forward_a, multiply, lambda k, arrivals: go_back(0, k, arrivals), there[0])
-
-    a_here = []
+    there.append(forward(0, 0, pieces[1], a_here[1]))
+    mixed = []
+    for k in range(PIECES):
+        mixed.append(multiply(k, there[k]))
+        if k + 2 < PIECES:
+            there.append(forward(0, 0, pieces[k + 2], a_here[k + 2]))
+
+    a_here, home = [], [turn(0, mixed[0])]
     for k, lanes in enumerate(pieces):
+        if k + 1 < PIECES:
+            home.append(turn(k + 1, mixed[k + 1]))
         arrive(home[k])
-        v = update_stream(0, lanes, stream)
+        v = update_stream(0, lanes, stream, yb_in.at[0], out_weights)
         stream[:, lanes] = v
         normed[:, lanes] = layer_norm(v.astype(F32)).astype(BF16)
         project(1, lanes, 0, normed, 0)
@@ -288,11 +301,11 @@
     def forward_b(q):
         return forward(1, 1, pieces[q], b_here[q])
 
-    home = in_steps(forward_b, multiply, lambda q, arrivals: go_back(1, q, arrivals), there[0])
+    home = in_steps(forward_b, multiply, go_back, there[0])
 
     for q, lanes in enumerate(pieces):
         arrive(home[q])
-        base = update_stream(1, lanes, stream_c).astype(F32)
+        base = update_stream(1, lanes, stream_c, wb_in, tri_out_ref[1]).astype(F32)
         v = layer_norm(base).astype(BF16)
         inner = dot(trans_in_ref[...], v, 0, 0)
         act = (jax.nn.silu(inner[:ffn]) * inner[ffn:]).astype(BF16)
@@ -334,7 +347,8 @@
             *buffers(2, nz, 2 * np_, tile),
             *buffers(2, np_, 2 * nz, tile),
             *buffers(2, np_, nz, tile),
-            *buffers(2, nz, np_, tile),
+            *buffers(nz, np_, tile),
+            *buffers(PIECES, nz, size // PIECES // nz, size),
             sem((z_banks,)), sem((z_banks,)), sem((x_banks,)), sem((x_banks,)),
         ],
         compiler_params=pltpu.CompilerParams(

time: 122 us -> 119 us (0.975)
  Pallas kernels: 120 us -> 117 us
    pallas_call x1, Pallas kernels: 120 us -> 117 us  [body(): pl.pallas_call(functools.partial(kernel, (nz, nx, ti, tk)), out_shape=jax...]
where the time goes in v3:
time: 119 us
  Pallas kernels  117 us (98%)
  local copies, waits for them, and re-layouts  1.69 us (1%)
    pallas_call x1, Pallas kernels, body(): pl.pallas_call(functools.partial(kernel, (nz, nx, ti, tk)), out_shape=jax...  117 us

profile of v3, /device:TPU:33, one launch (start us, length us, event | category | flops | bytes accessed | tf_op | source)
XLA Modules:
  0.0 119.2 jit_solution(11375113756783321294)
XLA Ops:
  0.7 116.9 %pairformer_block.1 = bf16[1152,128]{1,0:T(8,128)(2,1)} custom-call(s32[1]{0:T(128)S(6)} %copy.9.count_ref, bf16[1152,128]{1,0:T(8,128)(2,1)} %bitcast.3, bf16[2,128,512]{2,1,0:T(8,128)(2,1)} %tri_in_ref.1, bf16[2,128,128]{2,1,0:T(8,128)(2,1)} %tri_gate_ref.1, bf16[2,128,128]{2,1,0:T(8,128)(2,1)} %tri_out_ref.1, bf16[128,1024]{1,0:T(8,128)(2,1)} %trans_in_ref.1, ...), custom_call_target="tpu_custom_call" | custom-call | tf_op jit(solution)/shard_map/pairformer_block/pallas_call | solution.py:334
  117.5 1.7 %copy.10 = bf16[12,96,128]{2,1,0:T(8,128)(2,1)} copy(bf16[12,96,128]{2,1,0:T(8,128)(2,1)} %bitcast.2) | data formatting | bytes 589824

commit v4 on v3

--- a/solution.py
+++ b/solution.py
@@ -37,7 +37,9 @@
 
 
 def kernel(
-    dims, count_ref, pair_ref, tri_in_ref, tri_gate_ref, tri_out_ref, trans_in_ref, trans_out_ref, out_ref,
+    dims, count_ref, pair_hbm, tri_in_hbm, tri_gate_hbm, tri_out_hbm, trans_in_hbm, trans_out_hbm, out_hbm,
+    out_ref, stores,
+    pair_ref, tri_in_ref, tri_gate_ref, tri_out_ref, trans_in_ref, trans_out_ref, loads,
     stream, stream_c, normed, normed_c, gate, keep, left, right, turned, right_c,
     w_out, w_in, y_out, y_in, yb_out, yb_in, wb_out, wb_in, zc_out, zc_in,
     zs, zr, xs, xr,
@@ -45,9 +47,9 @@
     nz, nx, ti, tk = dims
     nc = CORES
     np_ = nc * nx
-    tile, chan = pair_ref.shape
-    hidden = tri_out_ref.shape[1]
-    ffn = trans_out_ref.shape[0]
+    tile, chan = pair_hbm.shape
+    hidden = tri_out_hbm.shape[1]
+    ffn = trans_out_hbm.shape[0]
     size = nx * tk
     z, c, x = lax.axis_index("row_0"), lax.axis_index("row_1"), lax.axis_index("col")
     me = c * nx + x
@@ -77,6 +79,12 @@
         pl.semaphore_signal(barrier, inc=1, device_id=at_z(z_peer(d)), device_id_type=MESH)
     for o in others:
         pl.semaphore_signal(barrier, inc=1, device_id=at_x(o), device_id_type=MESH)
+
+    sources = (pair_hbm, tri_in_hbm, tri_gate_hbm, tri_out_hbm, trans_in_hbm, trans_out_hbm)
+    targets = (pair_ref, tri_in_ref, tri_gate_ref, tri_out_ref, trans_in_ref, trans_out_ref)
+    loading = [pltpu.make_async_copy(a, b, loads.at[n]) for n, (a, b) in enumerate(zip(sources, targets))]
+    for copies in loading:
+        copies.start()
 
     started = []
     used = {"z": 0, "x": 0}
@@ -216,6 +224,8 @@
         return [home[k] for k in range(PIECES)]
 
     b_here, a_here = [], []
+    loading[0].wait()
+    loading[1].wait()
     for k, lanes in enumerate(pieces):
         v = pair_ref[lanes, :].astype(F32).T
         stream[:, lanes] = v.astype(BF16)
@@ -227,6 +237,9 @@
     for lanes in pieces:
         project(0, lanes, 0, normed, 0)
         a_here.append(send_w(0, a_in, lanes))
+    for copies in loading[2:]:
+        copies.wait()
+
     to_x = one_hot((hidden, hidden), lambda r: (r & (nz - 1)) * np_ + (r >> lz))
     to_z = one_hot((hidden, hidden), lambda r: (r & (np_ - 1)) * nz + (r >> lp))
     order = one_hot((size, size), lambda r: (r & (nz - 1)) * (nc * ti) + (r >> lz))
@@ -311,8 +324,11 @@
         act = (jax.nn.silu(inner[:ffn]) * inner[ffn:]).astype(BF16)
         update = dot(trans_out_ref[...], act, 0, 0)
         result = (base + keep[1:2, lanes] * update).T.astype(BF16)
-        for i in range(ti):
-            out_ref[i * tk + q * part : i * tk + (q + 1) * part, :] = result[i * part : (i + 1) * part]
+        cols = slice(q * part, (q + 1) * part)
+        out_ref[:, cols, :] = result.reshape(ti, part, chan)
+        store = pltpu.make_async_copy(out_ref.at[:, cols, :], out_hbm.at[:, cols, :], stores.at[q])
+        store.start()
+        started.append(store)
 
     for copies in started:
         copies.wait()
@@ -324,19 +340,22 @@
     nz, nx = lax.axis_size("row_0"), lax.axis_size("col")
     np_ = CORES * nx
     tile, size = ti * tk, nx * tk
-    vmem = pl.BlockSpec(memory_space=pltpu.VMEM)
+    hbm = pl.BlockSpec(memory_space=pltpu.HBM)
+    given = (pair.reshape(tile, chan), tri_in, tri_gate, tri_out, trans_in, trans_out)
     sem = pltpu.SemaphoreType.DMA
 
     def buffers(*shape):
         return [pltpu.VMEM(shape, BF16)] * 2
 
     z_banks, x_banks = 6 * PIECES, 1 + 5 * PIECES
-    out = pl.pallas_call(
+    return pl.pallas_call(
         functools.partial(kernel, (nz, nx, ti, tk)),
-        out_shape=jax.ShapeDtypeStruct((tile, chan), BF16),
-        in_specs=[pl.BlockSpec(memory_space=pltpu.SMEM)] + [vmem] * 6,
-        out_specs=vmem,
+        out_shape=jax.ShapeDtypeStruct((ti, tk, chan), BF16),
+        in_specs=[pl.BlockSpec(memory_space=pltpu.SMEM)] + [hbm] * len(given),
+        out_specs=hbm,
         scratch_shapes=[
+            pltpu.VMEM((ti, tk, chan), BF16), sem((PIECES,)),
+            *[pltpu.VMEM(v.shape, v.dtype) for v in given], sem((len(given),)),
             *buffers(chan, tile),
             *buffers(chan, tile),
             pltpu.VMEM((chan, tile), F32),
@@ -355,8 +374,7 @@
             collective_id=0, has_side_effects=True, vmem_limit_bytes=56 * 1024 * 1024
         ),
         name="pairformer_block",
-    )(token_count, pair.reshape(tile, chan), tri_in, tri_gate, tri_out, trans_in, trans_out)
-    return out.reshape(ti, tk, chan)
+    )(token_count, *given)
 
 
 def solution(mesh):

time: 119 us -> 117 us (0.983)
  Pallas kernels: 117 us -> 114 us
    pallas_call x1, Pallas kernels: 117 us -> 114 us  [body(): pl.pallas_call(functools.partial(kernel, (nz, nx, ti, tk)), out_shape=jax...]
where the time goes in v4:
time: 117 us; the launch traced here: 116 us
  Pallas kernels  114 us (97%)
  local copies, waits for them, and re-layouts  1.69 us (1%)
    pallas_call x1, Pallas kernels, body(): pl.pallas_call(functools.partial(kernel, (nz, nx, ti, tk)), out_shape=jax...  114 us

profile of v4, /device:TPU:33, one launch (start us, length us, event | category | flops | bytes accessed | tf_op | source)
XLA Modules:
  0.0 116.3 jit_solution(11258328189852461599)
XLA Ops:
  0.7 114.0 %pairformer_block.1 = bf16[12,96,128]{2,1,0:T(8,128)(2,1)} custom-call(s32[1]{0:T(128)S(6)} %copy.9.count_ref, bf16[1152,128]{1,0:T(8,128)(2,1)} %bitcast.1, bf16[2,128,512]{2,1,0:T(8,128)(2,1)} %tri_in_hbm.1, bf16[2,128,128]{2,1,0:T(8,128)(2,1)} %tri_gate_hbm.1, bf16[2,128,128]{2,1,0:T(8,128)(2,1)} %tri_out_hbm.1, bf16[128,1024]{1,0:T(8,128)(2,1)} %trans_in_hbm.1, ...), custom_call_target="tpu_custom_call" | custom-call | tf_op jit(solution)/shard_map/pairformer_block/pallas_call | solution.py:351
  114.6 1.7 %copy.10 = bf16[12,96,128]{2,1,0:T(8,128)(2,1)} copy(bf16[12,96,128]{2,1,0:T(8,128)(2,1)} %pairformer_block.1) | data formatting | bytes 589824
